TPU v7x, 32 devices: a whole 2x2x4 slice. The times are simulated.
32 devices in a mesh: row: 8 (over z, y), col: 4 (over x, core).
Axes of the slice: x: 2, y: 2, z: 4, core: 2. Of those that a mesh axis runs over, the one named last changes fastest.
Arguments:
- field: float32 [512, 64, 8, 512], P('row', 'col'), may hold values from -6 to 6
- modes: int32 [3, 256], replicated, may hold values from 0 to 511, as said below
Outputs:
- spectrum: float32 [64, 512, 8, 512], P(None, 'col', None, 'row')
- localized: float32 [512, 512], replicated
Inputs may be any that keep to these rules, and one draw needn't show every extreme that they name: `modes`: row 0 holds kx in 0 to 255, row 1 ky in 0 to 511, row 2 kz in 0 to 63; triples may repeat.
All inputs are finite; a program needn't handle non-finite values.
Results may differ from a plain program's by a relative error of at most 0.00013.
Values sent between devices are 32-bit elements; how exact they have to be, the bound alone decides.
A program may use at most 192 MiB of HBM per device.

v0:
```python
import math
import jax
import jax.numpy as jnp
from jax import lax
from jax.sharding import PartitionSpec as P

NX = 512
NY = 512
NZ = 64
REACH = 64
highest = lax.Precision.HIGHEST


def tables(length, count):
    points = lax.iota(jnp.int32, length)
    waves = lax.iota(jnp.int32, count)
    phase = points[:, None] * waves[None, :] % length
    angle = phase.astype(jnp.float32) * (2.0 * math.pi / length)
    return (jnp.cos(angle), jnp.sin(angle))


def rotation(count):
    source = lax.iota(jnp.int32, count)[:, None]
    target = lax.iota(jnp.int32, count)[None, :]
    even_out = target % 2 == 0
    plus = jnp.logical_and(source == target + 1, even_out).astype(jnp.float32)
    minus = jnp.logical_and(source + 1 == target, jnp.logical_not(even_out)).astype(jnp.float32)
    return plus - minus


def taper_of(modes, size_y, size_z, reach):
    first = modes[0].astype(jnp.float32)
    second = jnp.where(modes[1] < size_y // 2, modes[1], modes[1] - size_y).astype(jnp.float32)
    third = jnp.where(modes[2] < size_z // 2, modes[2], modes[2] - size_z).astype(jnp.float32)
    first = jnp.concatenate([first, first])
    second = jnp.concatenate([second, second])
    third = jnp.concatenate([third, third])
    dist = (first[:, None] - first[None, :]) ** 2 + (second[:, None] - second[None, :]) ** 2
    dist = dist + (third[:, None] - third[None, :]) ** 2
    return jnp.exp(-dist / (2.0 * reach * reach))


def y_transform(lines):
    length = lines.shape[0]
    cos_y, sin_y = tables(length, length)
    plain = jnp.einsum("ky,yzmq->kzmq", cos_y, lines, precision=highest)
    turned = jnp.einsum("ky,yzmq->kzmq", sin_y, lines, precision=highest)
    return plain + jnp.einsum("kzmq,qp->kzmp", turned, rotation(lines.shape[-1]), precision=highest)


def per_device(field, modes):
    members = field.shape[2]
    width = field.shape[3]
    cos_x, sin_x = tables(width, width // 2)
    x_table = jnp.stack([cos_x, -sin_x], axis=2).reshape(width, width)
    lines = jnp.einsum("yzmx,xq->yzmq", field, x_table, precision=highest)
    gathered = lax.all_to_all(lines, "row", split_axis=3, concat_axis=0, tiled=True)
    ytrans = y_transform(gathered)
    levels = lax.all_to_all(ytrans, "col", split_axis=0, concat_axis=1, tiled=True)
    depth = levels.shape[1]
    cos_z, sin_z = tables(depth, depth)
    plain = jnp.einsum("kz,yzmq->kymq", cos_z, levels, precision=highest)
    turned = jnp.einsum("kz,yzmq->kymq", sin_z, levels, precision=highest)
    combined = plain + jnp.einsum(
        "kymq,qp->kymp", turned, rotation(levels.shape[-1]), precision=highest
    )
    factor = 1.0 / math.sqrt(NX * NY * NZ)
    spectrum = combined * factor
    local_y = spectrum.shape[1]
    local_q = spectrum.shape[3]
    row_start = lax.axis_index("row") * local_q
    col_start = lax.axis_index("col") * local_y
    flat = spectrum.reshape(depth * local_y, members, local_q)
    offset = modes[1] - col_start
    inside_y = jnp.logical_and(offset >= 0, offset < local_y).astype(jnp.float32)
    index = modes[2] * local_y + jnp.clip(offset, 0, local_y - 1)
    picked_rows = flat[index]
    target = 2 * modes[0] - row_start
    columns = lax.iota(jnp.int32, local_q)[None, :]
    choose = jnp.stack([columns == target[:, None], columns == target[:, None] + 1], axis=2).astype(
        jnp.float32
    )
    choose = choose * inside_y[:, None, None]
    partial_value = jnp.einsum("smq,sqc->mcs", picked_rows, choose, precision=highest).reshape(
        members, -1
    )
    coef = lax.psum(partial_value, ("row", "col"))
    anomaly = coef - jnp.mean(coef, axis=0, keepdims=True)
    cov = jnp.dot(anomaly.T, anomaly, precision=highest) / (members - 1)
    localized = cov * taper_of(modes, NY, NZ, REACH)
    return (spectrum, localized)


def solution(mesh):
    placed = (P("row", "col", None, None), P())
    return jax.shard_map(
        per_device,
        mesh=mesh,
        in_specs=placed,
        out_specs=(P(None, "col", None, "row"), P()),
        check_vma=False,
    )
```

profile of v0, /device:TPU:0, one launch (start us, length us, event | category | flops | bytes accessed | tf_op | source)
XLA Modules:
  0.0 1293.4 jit_solution(5573586038033272029)
XLA Ops:
  4.6 40.4 %fusion.5 = f32[64,16,8,512]{3,0,2,1:T(8,128)} fusion(f32[64,16,8,512]{3,2,1,0:T(8,128)} %param.2, f32[512,512]{0,1:T(8,128)S(1)} %reshape.252), kind=kOutput, calls=%fused_computation.9 | convolution fusion | flops 25769803776 | bytes 34603008 | tf_op jit(solution)/shard_map/yzmx,xq->yzmq/dot_general | solution.py:56
  45.0 30.4 %copy.32 = f32[64,16,8,512]{0,2,1,3:T(8,128)} copy(f32[64,16,8,512]{3,0,2,1:T(8,128)} %fusion.5) | data formatting | bytes 33554432 | tf_op jit(solution)/shard_map/yzmx,xq->yzmq/dot_general | solution.py:56
  75.4 25.7 %reshape.273 = f32[8,1,524288]{2,1,0:T(1,128)} reshape(f32[512,16,8,64]{3,2,1,0:T(8,128)} %bitcast.65) | data formatting | bytes 33554432
  101.1 7.3 all-to-all-start
  108.4 363.1 %all-to-all-done = f32[8,1,524288]{2,1,0:T(1,128)} async-done(((f32[8,1,524288]{2,1,0:T(1,128)}), f32[8,1,524288]{2,1,0:T(1,128)}, u32[]{:S(2)}, u32[]{:S(2)}) %all-to-all-start) | async-done | bytes 16777248 | tf_op jit(solution)/shard_map/all_to_all | solution.py:57
  472.0 50.5 %reduce = f32[8,524288]{1,0:T(8,128)} reduce(f32[8,1,524288]{2,1,0:T(1,128)} %all-to-all-done, f32[]{:T(128)} %broadcast.368), dimensions={1}, to_apply=%all_to_all.26.reduce_sub_computation | reduce | bytes 33554436 | tf_op jit(solution)/shard_map/all_to_all | solution.py:57
  522.5 30.2 %reshape.274 = f32[512,16,8,64]{3,2,1,0:T(8,128)} reshape(f32[8,524288]{1,0:T(8,128)} %reduce) | data formatting | bytes 33554432
  552.7 31.9 %copy.60 = f32[64,16,8,8,64]{0,3,4,2,1:T(8,128)} copy(f32[64,16,8,8,64]{0,2,1,4,3:T(8,128)} %bitcast.67) | data formatting | bytes 33554432 | tf_op jit(solution)/shard_map/all_to_all | solution.py:57
  584.6 27.6 %reshape.264 = f32[512,8192]{0,1:T(8,128)} reshape(f32[8,64,16,8,64]{1,0,4,3,2:T(8,128)} %bitcast.68) | data formatting | bytes 33554432
  612.2 46.3 %fusion.15 = f32[512,8192]{0,1} fusion(f32[512,8192]{0,1:T(8,128)} %reshape.264), kind=kOutput, calls=%fused_computation.23 | convolution fusion | flops 25773473792 | bytes 33554432
  658.5 40.8 %fusion.13 = f32[512,8192]{0,1} fusion(f32[512,8192]{0,1:T(8,128)S(1)} %copy-done), kind=kOutput, calls=%fused_computation.21 | convolution fusion | flops 25773473792 | bytes 33554432
  699.3 22.7 %convolution_add_fusion = f32[512,16,8,64]{0,3,2,1:T(8,128)} fusion(f32[512,16,8,64]{0,3,2,1:T(8,128)} %bitcast.69, f32[512,16,8,64]{0,3,2,1:T(8,128)} %bitcast.70, s32[64]{0:T(128)S(1)} %iota_add_fusion, pred[64]{0:T(512)(128)(4,1)S(1)} %get-tuple-element.17, pred[64]{0:T(512)(128)(4,1)S(1)} %get-tuple-element.16), kind=kOutput, calls=%fused_computation.8 | convolution fusion | flops 3225448448 | bytes 50332032 | tf_op jit(solution)/shard_map/kzmq,qp->kzmp/dot_general | solution.py:48
  721.9 30.4 %copy.34 = f32[512,16,8,64]{3,2,1,0:T(8,128)} copy(f32[512,16,8,64]{0,3,2,1:T(8,128)} %convolution_add_fusion) | data formatting | bytes 33554432 | tf_op jit(solution)/shard_map/add | solution.py:48
  752.4 42.3 %reshape.275 = f32[4,1,1048576]{2,1,0:T(1,128)} reshape(f32[512,16,8,64]{3,2,1,0:T(8,128)} %copy.34) | data formatting | bytes 33554432
  802.1 182.7 %all-to-all-done.1 = f32[4,1,1048576]{2,1,0:T(1,128)} async-done(((f32[4,1,1048576]{2,1,0:T(1,128)}), f32[4,1,1048576]{2,1,0:T(1,128)}, u32[]{:S(2)}, u32[]{:S(2)}) %all-to-all-start.1) | async-done | bytes 16777248 | tf_op jit(solution)/shard_map/all_to_all | solution.py:59
  984.8 54.6 %reduce.1 = f32[4,1048576]{1,0:T(4,128)} reduce(f32[4,1,1048576]{2,1,0:T(1,128)} %all-to-all-done.1, f32[]{:T(128)} %broadcast.368), dimensions={1}, to_apply=%all_to_all.30.reduce_sub_computation | reduce | bytes 33554436 | tf_op jit(solution)/shard_map/all_to_all | solution.py:59
  1039.4 55.4 %reshape.276 = f32[512,16,8,64]{3,2,1,0:T(8,128)} reshape(f32[4,1048576]{1,0:T(4,128)} %reduce.1) | data formatting | bytes 33554432
  1094.8 24.7 %copy.35 = f32[4,128,16,8,64]{1,2,0,4,3:T(8,128)} copy(f32[4,128,16,8,64]{4,3,2,1,0:T(8,128)} %bitcast.66) | data formatting | bytes 33554432 | tf_op jit(solution)/shard_map/all_to_all | solution.py:59
  1119.5 21.7 %fusion.32 = f32[64,128,8,64]{1,0,3,2:T(8,128)} fusion(f32[128,64,8,64]{0,1,3,2:T(8,128)} %bitcast.63), kind=kOutput, calls=%fused_computation.48 | convolution fusion | flops 3221282816 | bytes 33554432 | tf_op jit(solution)/shard_map/kz,yzmq->kymq/dot_general | solution.py:63
  1141.2 36.6 %fusion.1 = f32[64,128,8,64]{1,3,2,0:T(8,128)} fusion(f32[64,128,8,64]{1,0,3,2:T(8,128)} %fusion.32, s32[64]{0:T(128)S(1)} %iota_add_fusion, pred[64]{0:T(512)(128)(4,1)S(1)} %get-tuple-element.17, pred[64]{0:T(512)(128)(4,1)S(1)} %get-tuple-element.16), kind=kOutput, calls=%fused_computation.4 | convolution fusion | flops 3221254144 | bytes 33554816 | tf_op jit(solution)/shard_map/kymq,qp->kymp/dot_general | solution.py:64
  1177.8 35.2 %fusion = f32[64,128,8,64]{1,0,3,2:T(8,128)} fusion(f32[64,128,8,64]{1,3,2,0:T(8,128)} %fusion.1, f32[128,64,8,64]{0,1,3,2:T(8,128)} %bitcast.64), kind=kOutput, calls=%fused_computation.3 | convolution fusion | flops 3229671424 | bytes 50331648 | tf_op jit(solution)/shard_map/kz,yzmq->kymq/dot_general | solution.py:62
  1213.0 20.0 %copy.47 = f32[64,128,8,64]{3,2,1,0:T(8,128)} copy(f32[64,128,8,64]{1,0,3,2:T(8,128)} %fusion) | data formatting | bytes 33554432 | tf_op jit(solution)/shard_map/reshape | solution.py:73
  1233.0 16.0 %copy.41 = f32[64,128,8,64]{1,3,2,0:T(8,128)} copy(f32[64,128,8,64]{1,0,3,2:T(8,128)} %fusion) | data formatting | bytes 33554432
  1253.3 37.6 %psum.7 = f32[8,512]{1,0:T(8,128)S(1)} all-reduce(f32[8,512]{1,0:T(8,128)S(1)} %bitcast.72), channel_id=1, replica_groups=mesh['row'=8,'col'=4] {'row','col'}, use_global_device_ids=true, to_apply=%region_0.1 | all-reduce | flops 4096 | bytes 32768 | tf_op jit(solution)/shard_map/psum | solution.py:87
  (30 shorter events, 18.4 us)
Async XLA Ops:
  101.1 370.4 %all-to-all-start = ((f32[8,1,524288]{2,1,0:T(1,128)}), f32[8,1,524288]{2,1,0:T(1,128)}, u32[]{:S(2)}, u32[]{:S(2)}) async-start(f32[8,1,524288]{2,1,0:T(1,128)} %reshape.273), calls=%async_computation | async-start | bytes 33554432 | tf_op jit(solution)/shard_map/all_to_all | solution.py:57
  612.2 46.3 %copy-start = (f32[512,8192]{0,1:T(8,128)S(1)}, f32[512,8192]{0,1:T(8,128)}, u32[]{:S(2)}) copy-start(f32[512,8192]{0,1:T(8,128)} %reshape.264) | copy-start | bytes 50331652
  794.6 7.1 copy-start.1
  794.6 190.1 %all-to-all-start.1 = ((f32[4,1,1048576]{2,1,0:T(1,128)}), f32[4,1,1048576]{2,1,0:T(1,128)}, u32[]{:S(2)}, u32[]{:S(2)}) async-start(f32[4,1,1048576]{2,1,0:T(1,128)} %reshape.275), calls=%async_computation.1 | async-start | bytes 33554432 | tf_op jit(solution)/shard_map/all_to_all | solution.py:59
where the time goes:
time: 1300 us; the launch traced here: 1290 us
  waiting for transfers between devices  546 us (42%)
  local copies, waits for them, and re-layouts  340 us (26%)
  matrix products  248 us (19%)
  other arithmetic  107 us (8%)
  blocking collectives  37.6 us (3%)
  starting transfers between devices  14.4 us (1%)
    all_to_all x1, waiting for transfers between devices, per_device(): lax.all_to_all(lines, 'row', split_axis=3, concat_axis=0, tiled=True)  363 us
    unnamed x11, local copies, waits for them, and re-layouts  197 us
    all_to_all x1, waiting for transfers between devices, per_device(): lax.all_to_all(ytrans, 'col', split_axis=0, concat_axis=1, tiled=True)  183 us
    unnamed x2, matrix products  87 us
    all_to_all x1, other arithmetic, per_device(): lax.all_to_all(ytrans, 'col', split_axis=0, concat_axis=1, tiled=True)  54.6 us
    all_to_all x1, other arithmetic, per_device(): lax.all_to_all(lines, 'row', split_axis=3, concat_axis=0, tiled=True)  50.5 us
    dot_general x1, matrix products, per_device(): lines = jnp.einsum('yzmx,xq->yzmq', field, x_table, precision=highest)  40.4 us
    psum x1, blocking collectives, per_device(): coef = lax.psum(partial_value, ('row', 'col'))  37.6 us
  transfers between devices with their start and end apart: 2, of which 2 were waited for; matrix products, arithmetic and copies ran while one was open for 0% of the time, Pallas kernels for 0%

commit v1 on v0

--- a/solution.py
+++ b/solution.py
@@ -56,7 +56,10 @@
     lines = jnp.einsum("yzmx,xq->yzmq", field, x_table, precision=highest)
     gathered = lax.all_to_all(lines, "row", split_axis=3, concat_axis=0, tiled=True)
     ytrans = y_transform(gathered)
-    levels = lax.all_to_all(ytrans, "col", split_axis=0, concat_axis=1, tiled=True)
+    levels = jnp.concatenate(
+        lax.all_to_all(jnp.stack(jnp.split(ytrans, lax.axis_size("col"), axis=0)), "col", 0, 0),
+        axis=1,
+    )
     depth = levels.shape[1]
     cos_z, sin_z = tables(depth, depth)
     plain = jnp.einsum("kz,yzmq->kymq", cos_z, levels, precision=highest)

time: 1300 us -> 1130 us (0.87)
  local copies, waits for them, and re-layouts: 340 us -> 193 us
  other arithmetic: 107 us -> 59 us
  matrix products: 248 us -> 270 us
    unnamed x11 -> x9, local copies, waits for them, and re-layouts: 197 us -> 99.6 us
    all_to_all x1 -> x0, other arithmetic: 54.6 us -> none  [per_device(): lax.all_to_all(ytrans, 'col', split_axis=0, concat_axis=1, tiled=True)]
    add x1 -> x0, local copies, waits for them, and re-layouts: 30.4 us -> none  [y_transform(): plain + jnp.einsum('kzmq,qp->kzmp', turned, rotation(lines.shape[-1]), pr...]
    all_to_all x1 -> x0, local copies, waits for them, and re-layouts: 24.7 us -> none  [per_device(): lax.all_to_all(ytrans, 'col', split_axis=0, concat_axis=1, tiled=True)]
where the time goes in v1:
time: 1130 us; the launch traced here: 1120 us
  waiting for transfers between devices  546 us (48%)
  matrix products  270 us (24%)
  local copies, waits for them, and re-layouts  193 us (17%)
  other arithmetic  59 us (5%)
  blocking collectives  37.7 us (3%)
  starting transfers between devices  14.4 us (1%)
    all_to_all x1, waiting for transfers between devices, per_device(): lax.all_to_all(lines, 'row', split_axis=3, concat_axis=0, tiled=True)  363 us
    all_to_all x1, waiting for transfers between devices, per_device(): lax.all_to_all(jnp.stack(jnp.split(ytrans, lax.axis_size('col'), axis=0))...  183 us
    unnamed x9, local copies, waits for them, and re-layouts  99.6 us
    unnamed x2, matrix products  86.8 us
    all_to_all x1, other arithmetic, per_device(): lax.all_to_all(lines, 'row', split_axis=3, concat_axis=0, tiled=True)  50.5 us
    dot_general x1, matrix products, per_device(): plain = jnp.einsum('kz,yzmq->kymq', cos_z, levels, precision=highest)  46.7 us
    dot_general x1, matrix products, per_device(): lines = jnp.einsum('yzmx,xq->yzmq', field, x_table, precision=highest)  40.4 us
    psum x1, blocking collectives, per_device(): coef = lax.psum(partial_value, ('row', 'col'))  37.7 us
  transfers between devices with their start and end apart: 2, of which 2 were waited for; matrix products, arithmetic and copies ran while one was open for 0% of the time, Pallas kernels for 0%

profile of v1, /device:TPU:0, one launch (start us, length us, event | category | flops | bytes accessed | tf_op | source)
XLA Modules:
  0.0 1121.5 jit_solution(13963024268899041357)
XLA Ops:
  4.3 40.4 %fusion.11 = f32[64,16,8,512]{3,0,2,1:T(8,128)} fusion(f32[64,16,8,512]{3,2,1,0:T(8,128)} %param.2, f32[512,512]{0,1:T(8,128)S(1)} %reshape.258), kind=kOutput, calls=%fused_computation.14 | convolution fusion | flops 25769803776 | bytes 34603008 | tf_op jit(solution)/shard_map/yzmx,xq->yzmq/dot_general | solution.py:56
  44.6 30.4 %copy.32 = f32[64,16,8,512]{0,2,1,3:T(8,128)} copy(f32[64,16,8,512]{3,0,2,1:T(8,128)} %fusion.11) | data formatting | bytes 33554432 | tf_op jit(solution)/shard_map/yzmx,xq->yzmq/dot_general | solution.py:56
  75.1 25.9 %reshape.281 = f32[8,1,524288]{2,1,0:T(1,128)} reshape(f32[512,16,8,64]{3,2,1,0:T(8,128)} %bitcast.68) | data formatting | bytes 33554432
  101.0 7.3 all-to-all-start
  108.3 363.0 %all-to-all-done = f32[8,1,524288]{2,1,0:T(1,128)} async-done(((f32[8,1,524288]{2,1,0:T(1,128)}), f32[8,1,524288]{2,1,0:T(1,128)}, u32[]{:S(2)}, u32[]{:S(2)}) %all-to-all-start) | async-done | bytes 16777248 | tf_op jit(solution)/shard_map/all_to_all | solution.py:57
  471.8 50.5 %reduce = f32[8,524288]{1,0:T(8,128)} reduce(f32[8,1,524288]{2,1,0:T(1,128)} %all-to-all-done, f32[]{:T(128)} %broadcast.368), dimensions={1}, to_apply=%all_to_all.16.reduce_sub_computation | reduce | bytes 33554436 | tf_op jit(solution)/shard_map/all_to_all | solution.py:57
  522.3 30.0 %reshape.282 = f32[512,16,8,64]{3,2,1,0:T(8,128)} reshape(f32[8,524288]{1,0:T(8,128)} %reduce) | data formatting | bytes 33554432
  552.3 31.9 %copy.66 = f32[64,16,8,8,64]{0,3,4,2,1:T(8,128)} copy(f32[64,16,8,8,64]{0,2,1,4,3:T(8,128)} %bitcast.69) | data formatting | bytes 33554432 | tf_op jit(solution)/shard_map/all_to_all | solution.py:57
  584.2 27.6 %reshape.272 = f32[512,8192]{0,1:T(8,128)} reshape(f32[8,64,16,8,64]{1,0,4,3,2:T(8,128)} %bitcast.70) | data formatting | bytes 33554432
  611.8 46.2 %fusion.21 = f32[512,8192]{0,1} fusion(f32[512,8192]{0,1:T(8,128)} %reshape.272), kind=kOutput, calls=%fused_computation.32 | convolution fusion | flops 25773473792 | bytes 33554432
  658.1 40.6 %fusion.19 = f32[512,8192]{0,1} fusion(f32[512,8192]{0,1:T(8,128)S(1)} %copy-done), kind=kOutput, calls=%fused_computation.30 | convolution fusion | flops 25773473792 | bytes 33554432
  698.7 22.7 %convolution_add_fusion = f32[512,16,8,64]{0,3,2,1:T(8,128)} fusion(f32[512,16,8,64]{0,3,2,1:T(8,128)} %bitcast.71, f32[512,16,8,64]{0,3,2,1:T(8,128)} %bitcast.72, s32[64]{0:T(128)S(1)} %iota_add_fusion, pred[64]{0:T(512)(128)(4,1)S(1)} %get-tuple-element.21, pred[64]{0:T(512)(128)(4,1)S(1)} %get-tuple-element.20), kind=kOutput, calls=%fused_computation.13 | convolution fusion | flops 3225448448 | bytes 50332032 | tf_op jit(solution)/shard_map/kzmq,qp->kzmp/dot_general | solution.py:48
  721.4 6.8 slice_bitcast_fusion.3
  728.2 6.2 pad_maximum_fusion
  734.5 7.1 all-to-all-start.1
  742.0 182.7 %all-to-all-done.1 = f32[4,128,16,8,64]{1,4,3,2,0:T(8,128)} async-done(((f32[4,128,16,8,64]{1,4,3,2,0:T(8,128)}), f32[4,128,16,8,64]{1,4,3,2,0:T(8,128)}, u32[]{:S(2)}, u32[]{:S(2)}) %all-to-all-start.1) | async-done | bytes 16777248 | tf_op jit(solution)/shard_map/all_to_all | solution.py:60
  924.6 33.2 %fusion.5 = f32[64,128,8,64]{1,0,3,2:T(8,128)} fusion(f32[128,64,8,64]{0,3,2,1:T(8,128)} %bitcast.15), kind=kOutput, calls=%fused_computation.9 | convolution fusion | flops 3221282816 | bytes 33554432 | tf_op jit(solution)/shard_map/kz,yzmq->kymq/dot_general | solution.py:66
  957.9 36.4 %fusion.1 = f32[64,128,8,64]{1,3,2,0:T(8,128)} fusion(f32[64,128,8,64]{1,0,3,2:T(8,128)} %fusion.5, s32[64]{0:T(128)S(1)} %iota_add_fusion, pred[64]{0:T(512)(128)(4,1)S(1)} %get-tuple-element.21, pred[64]{0:T(512)(128)(4,1)S(1)} %get-tuple-element.20), kind=kOutput, calls=%fused_computation.5 | convolution fusion | flops 3221254144 | bytes 33554816 | tf_op jit(solution)/shard_map/kymq,qp->kymp/dot_general | solution.py:67
  994.3 46.7 %fusion = f32[64,128,8,64]{1,0,3,2:T(8,128)} fusion(f32[64,128,8,64]{1,3,2,0:T(8,128)} %fusion.1, f32[128,64,8,64]{0,3,2,1:T(8,128)} %bitcast.15), kind=kOutput, calls=%fused_computation.4 | convolution fusion | flops 3229671424 | bytes 50331648 | tf_op jit(solution)/shard_map/kz,yzmq->kymq/dot_general | solution.py:65
  1041.0 20.0 %copy.47 = f32[64,128,8,64]{3,2,1,0:T(8,128)} copy(f32[64,128,8,64]{1,0,3,2:T(8,128)} %fusion) | data formatting | bytes 33554432 | tf_op jit(solution)/shard_map/reshape | solution.py:76
  1061.0 16.0 %copy.41 = f32[64,128,8,64]{1,3,2,0:T(8,128)} copy(f32[64,128,8,64]{1,0,3,2:T(8,128)} %fusion) | data formatting | bytes 33554432
  1077.0 2.3 gather_fusion
  1081.3 37.7 %psum.7 = f32[8,512]{1,0:T(8,128)S(1)} all-reduce(f32[8,512]{1,0:T(8,128)S(1)} %bitcast.74), channel_id=1, replica_groups=mesh['row'=8,'col'=4] {'row','col'}, use_global_device_ids=true, to_apply=%region_0.1 | all-reduce | flops 4096 | bytes 32768 | tf_op jit(solution)/shard_map/psum | solution.py:90
  1119.0 2.3 fusion.14
  (27 shorter events, 6.3 us)
Async XLA Ops:
  101.0 370.3 %all-to-all-start = ((f32[8,1,524288]{2,1,0:T(1,128)}), f32[8,1,524288]{2,1,0:T(1,128)}, u32[]{:S(2)}, u32[]{:S(2)}) async-start(f32[8,1,524288]{2,1,0:T(1,128)} %reshape.281), calls=%async_computation | async-start | bytes 33554432 | tf_op jit(solution)/shard_map/all_to_all | solution.py:57
  611.8 46.2 %copy-start = (f32[512,8192]{0,1:T(8,128)S(1)}, f32[512,8192]{0,1:T(8,128)}, u32[]{:S(2)}) copy-start(f32[512,8192]{0,1:T(8,128)} %reshape.272) | copy-start | bytes 50331652
  734.5 7.1 copy-start.1
  734.5 190.1 %all-to-all-start.1 = ((f32[4,128,16,8,64]{1,4,3,2,0:T(8,128)}), f32[4,128,16,8,64]{1,4,3,2,0:T(8,128)}, u32[]{:S(2)}, u32[]{:S(2)}) async-start(f32[4,128,16,8,64]{1,4,3,2,0:T(8,128)} %pad_maximum_fusion), calls=%async_computation.1 | async-start | bytes 33554432 | tf_op jit(solution)/shard_map/all_to_all | solution.py:60
